TPU v7x, 32 devices: a whole 2x2x4 slice. The times are simulated.
32 devices in a mesh: path: 16 (over z, x, core), shard: 2 (over y).
Axes of the slice: x: 2, y: 2, z: 4, core: 2. Of those that a mesh axis runs over, the one named last changes fastest.
Arguments:
- deltas: bfloat16 [16, 32, 4096], P('path', 'shard'), may hold values from -96 to 96
- momentum: float32 [16, 32, 4096], P(None, 'shard', 'path'), may hold values from -4 to 4
- path_module: int32 [16], replicated, may hold values from 0 to 15, as said below
Outputs:
- path_update: bfloat16 [16, 32, 4096], P('path', 'shard')
- new_momentum: float32 [16, 32, 4096], P(None, 'shard', 'path')
Inputs may be any that keep to these rules, and one draw needn't show every extreme that they name: `path_module`: every module is used by at least one and at most seven paths.
All inputs are finite; a program needn't handle non-finite values.
Results may differ from a plain program's by a relative error of at most 0.0004.
Values may be sent and summed in bfloat16 or wider, within the bound.
A program may use at most 64 MiB of HBM per device.

v0:
```python
import jax
import jax.numpy as jnp
from jax import lax
from jax.sharding import PartitionSpec as P

D = 4096
outer_rate = 0.7
momentum_rate = 0.9
clip_ratio = 2.0


def local(deltas, momentum, path_module):
    own_index = lax.axis_index("path")
    modules = momentum.shape[0]
    row_count = deltas.shape[1]
    onehot = (path_module[:, None] == jnp.arange(modules, dtype=jnp.int32)[None, :]).astype(
        jnp.float32
    )
    counts = jnp.sum(onehot, axis=0)
    own_module = lax.dynamic_index_in_dim(path_module, own_index, 0, keepdims=False)
    column_pieces = lax.all_to_all(deltas, "path", split_axis=2, concat_axis=0, tiled=True)
    totals = jnp.einsum(
        "pm,prc->mrc",
        onehot.astype(jnp.bfloat16),
        column_pieces,
        preferred_element_type=jnp.float32,
    )
    outer_grad = totals / counts[:, None, None]
    local_squares = jnp.sum(outer_grad * outer_grad, axis=(1, 2))
    norm_squares = lax.psum(local_squares, ("path", "shard"))
    limit = clip_ratio * jnp.sqrt(jnp.float32(row_count * lax.axis_size("shard") * D))
    shrink = jnp.minimum(1.0, limit / jnp.sqrt(norm_squares + 1e-06))
    clipped = outer_grad * shrink[:, None, None]
    new_momentum = momentum_rate * momentum + clipped
    outer_step = (outer_rate * (clipped + momentum_rate * new_momentum)).astype(jnp.bfloat16)
    gathered = lax.all_gather(outer_step, "path", axis=2, tiled=True)
    path_update = lax.dynamic_index_in_dim(gathered, own_module, 0, keepdims=True)
    return (path_update, new_momentum)


def solution(mesh):
    return jax.shard_map(
        local,
        mesh=mesh,
        in_specs=(P("path", "shard", None), P(None, "shard", "path"), P()),
        out_specs=(P("path", "shard", None), P(None, "shard", "path")),
        check_vma=False,
    )
```

profile of v0, /device:TPU:0, one launch (start us, length us, event | category | flops | bytes accessed | tf_op | source)
XLA Modules:
  0.0 145.2 jit_solution(7055501070345371449)
XLA Ops:
  7.2 4.3 %copy.8 = bf16[1,16,4096]{1,0,2:T(2,128)(2,1)S(1)} copy(bf16[1,16,4096]{2,1,0:T(8,128)(2,1)} %param.3) | data formatting | bytes 262144 | tf_op args[0]
  11.5 0.5 broadcast.26
  12.0 0.0 copy-start.1
  12.0 22.4 %reduce = bf16[4096,16]{1,0:T(8,128)(2,1)S(1)} reduce(bf16[4096,1,16]{2,1,0:T(2,128)(2,1)S(1)} %bitcast.25, bf16[]{:T(256)} %broadcast.26), dimensions={1}, to_apply=%bitcast.15.reduce_sub_computation | reduce | bytes 262146
  34.4 1.8 %reshape.8 = bf16[16,2,2048]{2,1,0:T(2,128)(2,1)} reshape(bf16[4096,16]{1,0:T(8,128)(2,1)S(1)} %reduce) | data formatting | bytes 262144
  36.2 7.4 %all-to-all-start = ((bf16[16,2,2048]{2,1,0:T(2,128)(2,1)}), bf16[16,2,2048]{2,1,0:T(2,128)(2,1)S(1)}, u32[]{:S(2)}, u32[]{:S(2)}) async-start(bf16[16,2,2048]{2,1,0:T(2,128)(2,1)} %reshape.8), calls=%async_computation | async-start | bytes 262144 | tf_op jit(solution)/shard_map/all_to_all | solution.py:21
  43.6 0.0 all-gather.2.cloned.1.call-start
  43.6 0.0 copy-done.1
  43.6 0.1 convert_reduce_fusion
  43.8 7.7 %all-to-all-done = bf16[16,2,2048]{2,1,0:T(2,128)(2,1)S(1)} async-done(((bf16[16,2,2048]{2,1,0:T(2,128)(2,1)}), bf16[16,2,2048]{2,1,0:T(2,128)(2,1)S(1)}, u32[]{:S(2)}, u32[]{:S(2)}) %all-to-all-start) | async-done | bytes 131104 | tf_op jit(solution)/shard_map/all_to_all | solution.py:21
  51.5 1.8 %reshape.9 = bf16[4096,1,16]{2,1,0:T(2,128)(2,1)S(1)} reshape(bf16[16,2,2048]{2,1,0:T(2,128)(2,1)S(1)} %all-to-all-done) | data formatting | bytes 262144
  53.3 0.0 copy-start
  53.3 2.0 %copy.9 = bf16[1,16,4096]{2,1,0:T(8,128)(2,1)S(1)} copy(bf16[1,16,4096]{1,0,2:T(2,128)(2,1)S(1)} %bitcast.26) | data formatting | bytes 262144 | tf_op jit(solution)/shard_map/all_to_all | solution.py:21
  55.3 0.3 multiply_reduce_fusion
  55.6 37.5 %psum.7 = f32[16]{0:T(128)S(1)} all-reduce(f32[16]{0:T(128)S(1)} %get-tuple-element.8), channel_id=1, replica_groups=mesh['path'=16,'shard'=2] {'path','shard'}, use_global_device_ids=true, to_apply=%region_2.3 | all-reduce | flops 16 | bytes 128 | tf_op jit(solution)/shard_map/psum | solution.py:30
  93.1 0.0 copy-done
  93.1 0.9 fusion
  94.0 0.0 all-gather.2.cloned.1.call-update
  94.0 0.6 dynamic_slice.8
  96.5 0.9 copy.12
  97.4 38.6 %all-gather.2.cloned.1.call-done = bf16[16,16,4096]{2,0,1:T(8,128)(2,1)} async-done(((bf16[16,16,256]{2,0,1:T(8,128)(2,1)}), bf16[16,16,4096]{2,0,1:T(8,128)(2,1)}) %all-gather.2.cloned.1.call-update) | async-done | bytes 2097168 | tf_op jit(solution)/shard_map/all_gather | solution.py:36
  136.0 1.5 %constant_dynamic-slice_fusion = bf16[1,16,4096]{2,0,1:T(2,128)(2,1)S(1)} fusion(bf16[16,16,4096]{2,0,1:T(8,128)(2,1)} %all-gather.2.cloned.1.call-done, s32[]{:T(128)S(6)} %select_n.9), kind=kLoop, calls=%fused_computation.12 | loop fusion | bytes 262148 | tf_op jit(solution)/shard_map/jit(dynamic_index_in_dim)/dynamic_slice | solution.py:37
  137.5 0.8 copy.11
  (2 shorter events, 0.0 us)
Async XLA Ops:
  12.0 31.6 %copy-start.1 = (s32[16]{0:T(128)S(1)}, s32[16]{0:T(128)}, u32[]{:S(2)}) copy-start(s32[16]{0:T(128)} %param.5) | copy-start | bytes 196
  36.2 15.3 %all-to-all-start = ((bf16[16,2,2048]{2,1,0:T(2,128)(2,1)}), bf16[16,2,2048]{2,1,0:T(2,128)(2,1)S(1)}, u32[]{:S(2)}, u32[]{:S(2)}) async-start(bf16[16,2,2048]{2,1,0:T(2,128)(2,1)} %reshape.8), calls=%async_computation | async-start | bytes 262144 | tf_op jit(solution)/shard_map/all_to_all | solution.py:21
  43.6 92.4 %all-gather.2.cloned.1.call-start = ((), (), s32[]{:S(2)}) async-start(), calls=%async_computation.1 | async-start | bytes 2228224 | tf_op jit(solution)/shard_map/all_gather | solution.py:36
  53.3 39.8 %copy-start = (f32[16,16,256]{2,1,0:T(8,128)S(1)}, f32[16,16,256]{2,1,0:T(8,128)}, u32[]{:S(2)}) copy-start(f32[16,16,256]{2,1,0:T(8,128)} %param.4) | copy-start | bytes 786436
Sparse Core Ops, SparseCore 0:
  94.1 41.7 all-gather.1
where the time goes:
time: 146 us; the launch traced here: 145 us
  waiting for transfers between devices  46.3 us (32%)
  blocking collectives  37.5 us (26%)
  other arithmetic  23.4 us (16%)
  between operations  16 us (11%)
  local copies, waits for them, and re-layouts  14.2 us (10%)
  starting transfers between devices  7.43 us (5%)
    all_gather x1, waiting for transfers between devices, local(): gathered = lax.all_gather(outer_step, 'path', axis=2, tiled=True)  38.6 us
    psum x1, blocking collectives, local(): norm_squares = lax.psum(local_squares, ('path', 'shard'))  37.5 us
    unnamed x1, other arithmetic  22.4 us
    unnamed x11, local copies, waits for them, and re-layouts  10.1 us
    all_to_all x1, waiting for transfers between devices, local(): lax.all_to_all(deltas, 'path', split_axis=2, concat_axis=0, tiled=True)  7.73 us
    all_to_all x1, starting transfers between devices, local(): lax.all_to_all(deltas, 'path', split_axis=2, concat_axis=0, tiled=True)  7.39 us
  transfers between devices with their start and end apart: 2, of which 2 were waited for; matrix products, arithmetic and copies ran while one was open for 1% of the time, Pallas kernels for 0%

commit v1 on v0

--- a/solution.py
+++ b/solution.py
@@ -1,3 +1,4 @@
+import functools
 import jax
 import jax.numpy as jnp
 from jax import lax
@@ -7,6 +8,22 @@
 outer_rate = 0.7
 momentum_rate = 0.9
 clip_ratio = 2.0
+
+
+def link_the_sides(arr_in, which_axis):
+    width = lax.axis_size(which_axis)
+    leaves = tuple(((ix, (ix + 1) % width) for ix in range(width)))
+
+    def _bring_columns(mid_arr):
+        if len(mid_arr) == width:
+            return mid_arr
+        return _bring_columns([lax.ppermute(mid_arr[0], which_axis, leaves), *mid_arr])
+
+    vec_out = jnp.concatenate(_bring_columns([arr_in]), axis=2)
+    return jnp.roll(vec_out, (lax.axis_index(which_axis) + 1) * arr_in.shape[2], 2)
+
+
+number_cube_on = functools.partial(link_the_sides, which_axis="path")
 
 
 def local(deltas, momentum, path_module):
@@ -33,7 +50,7 @@
     clipped = outer_grad * shrink[:, None, None]
     new_momentum = momentum_rate * momentum + clipped
     outer_step = (outer_rate * (clipped + momentum_rate * new_momentum)).astype(jnp.bfloat16)
-    gathered = lax.all_gather(outer_step, "path", axis=2, tiled=True)
+    gathered = number_cube_on(outer_step)
     path_update = lax.dynamic_index_in_dim(gathered, own_module, 0, keepdims=True)
     return (path_update, new_momentum)
 

time: 146 us -> 196 us (1.34)
  waiting for transfers between devices: 46.3 us -> 111 us
  between operations: 16 us -> 2.95 us
    ppermute x0 -> x15, waiting for transfers between devices: none -> 103 us  [_bring_columns(): lax.ppermute(mid_arr[0], which_axis, leaves)]
    all_gather x1 -> x0, waiting for transfers between devices: 38.6 us -> none  [local(): gathered = lax.all_gather(outer_step, 'path', axis=2, tiled=True)]
    unnamed x11 -> x42, local copies, waits for them, and re-layouts: 10.1 us -> 10.4 us
  transfers between devices with their start and end apart: 2 -> 16, of which waited for: 2 -> 16; matrix products, arithmetic and copies ran while one was open for 1% -> 1% of each run, Pallas kernels for 0% -> 0%
where the time goes in v1:
time: 196 us; the launch traced here: 195 us
  waiting for transfers between devices  111 us (57%)
  blocking collectives  37.5 us (19%)
  other arithmetic  22.7 us (12%)
  local copies, waits for them, and re-layouts  13.5 us (7%)
  starting transfers between devices  7.48 us (4%)
  between operations  2.95 us (2%)
    ppermute x15, waiting for transfers between devices, _bring_columns(): lax.ppermute(mid_arr[0], which_axis, leaves)  103 us
    psum x1, blocking collectives, local(): norm_squares = lax.psum(local_squares, ('path', 'shard'))  37.5 us
    unnamed x1, other arithmetic  22.4 us
    unnamed x42, local copies, waits for them, and re-layouts  10.4 us
    all_to_all x1, waiting for transfers between devices, local(): lax.all_to_all(deltas, 'path', split_axis=2, concat_axis=0, tiled=True)  7.78 us
    all_to_all x1, starting transfers between devices, local(): lax.all_to_all(deltas, 'path', split_axis=2, concat_axis=0, tiled=True)  7.39 us
  transfers between devices with their start and end apart: 16, of which 16 were waited for; matrix products, arithmetic and copies ran while one was open for 1% of the time, Pallas kernels for 0%

profile of v1, /device:TPU:0, one launch (start us, length us, event | category | flops | bytes accessed | tf_op | source)
XLA Modules:
  0.0 195.1 jit_solution(15357455674444460298)
XLA Ops:
  0.6 0.0 copy-start.1
  0.6 4.3 %copy.8 = bf16[1,16,4096]{1,0,2:T(2,128)(2,1)S(1)} copy(bf16[1,16,4096]{2,1,0:T(8,128)(2,1)} %param.3) | data formatting | bytes 262144 | tf_op args[0]
  5.0 0.5 broadcast.27
  5.5 22.4 %reduce = bf16[4096,16]{1,0:T(8,128)(2,1)S(1)} reduce(bf16[4096,1,16]{2,1,0:T(2,128)(2,1)S(1)} %bitcast.25, bf16[]{:T(256)} %broadcast.27), dimensions={1}, to_apply=%bitcast.15.reduce_sub_computation | reduce | bytes 262146
  27.9 0.0 copy-start
  27.9 1.8 reshape.8
  29.7 7.4 %all-to-all-start = ((bf16[16,2,2048]{2,1,0:T(2,128)(2,1)}), bf16[16,2,2048]{2,1,0:T(2,128)(2,1)S(1)}, u32[]{:S(2)}, u32[]{:S(2)}) async-start(bf16[16,2,2048]{2,1,0:T(2,128)(2,1)} %reshape.8), calls=%async_computation | async-start | bytes 262144 | tf_op jit(solution)/shard_map/all_to_all | solution.py:38
  37.1 0.1 convert_reduce_fusion
  37.2 7.8 %all-to-all-done = bf16[16,2,2048]{2,1,0:T(2,128)(2,1)S(1)} async-done(((bf16[16,2,2048]{2,1,0:T(2,128)(2,1)}), bf16[16,2,2048]{2,1,0:T(2,128)(2,1)S(1)}, u32[]{:S(2)}, u32[]{:S(2)}) %all-to-all-start) | async-done | bytes 131104 | tf_op jit(solution)/shard_map/all_to_all | solution.py:38
  45.0 1.8 reshape.9
  46.8 2.0 %copy.9 = bf16[1,16,4096]{2,1,0:T(8,128)(2,1)S(1)} copy(bf16[1,16,4096]{1,0,2:T(2,128)(2,1)S(1)} %bitcast.26) | data formatting | bytes 262144 | tf_op jit(solution)/shard_map/all_to_all | solution.py:38
  48.8 0.3 multiply_reduce_fusion
  49.1 37.5 %psum.7 = f32[16]{0:T(128)S(1)} all-reduce(f32[16]{0:T(128)S(1)} %get-tuple-element.8), channel_id=1, replica_groups=mesh['path'=16,'shard'=2] {'path','shard'}, use_global_device_ids=true, to_apply=%region_2.3 | all-reduce | flops 16 | bytes 128 | tf_op jit(solution)/shard_map/psum | solution.py:47
  86.6 0.2 fusion
  86.8 0.1 collective-permute-start
  86.8 7.1 %collective-permute-done = bf16[16,16,256]{2,0,1:T(8,128)(2,1)S(1)} collective-permute-done((bf16[16,16,256]{2,0,1:T(8,128)(2,1)S(1)}, bf16[16,16,256]{2,0,1:T(8,128)(2,1)S(1)}, u32[]{:S(2)}, u32[]{:S(2)}) %collective-permute-start) | collective-permute-done | bytes 131104 | tf_op jit(solution)/shard_map/ppermute | solution.py:20
  93.9 0.0 collective-permute-start.1
  93.9 7.1 %collective-permute-done.1 = bf16[16,16,256]{2,0,1:T(8,128)(2,1)S(1)} collective-permute-done((bf16[16,16,256]{2,0,1:T(8,128)(2,1)S(1)}, bf16[16,16,256]{2,0,1:T(8,128)(2,1)S(1)}, u32[]{:S(2)}, u32[]{:S(2)}) %collective-permute-start.1) | collective-permute-done | bytes 131104 | tf_op jit(solution)/shard_map/ppermute | solution.py:20
  101.0 0.0 collective-permute-start.2
  101.0 7.1 %collective-permute-done.2 = bf16[16,16,256]{2,0,1:T(8,128)(2,1)S(1)} collective-permute-done((bf16[16,16,256]{2,0,1:T(8,128)(2,1)S(1)}, bf16[16,16,256]{2,0,1:T(8,128)(2,1)S(1)}, u32[]{:S(2)}, u32[]{:S(2)}) %collective-permute-start.2) | collective-permute-done | bytes 131104 | tf_op jit(solution)/shard_map/ppermute | solution.py:20
  108.1 0.0 collective-permute-start.3
  108.1 7.1 %collective-permute-done.3 = bf16[16,16,256]{2,0,1:T(8,128)(2,1)S(1)} collective-permute-done((bf16[16,16,256]{2,0,1:T(8,128)(2,1)S(1)}, bf16[16,16,256]{2,0,1:T(8,128)(2,1)S(1)}, u32[]{:S(2)}, u32[]{:S(2)}) %collective-permute-start.3) | collective-permute-done | bytes 131104 | tf_op jit(solution)/shard_map/ppermute | solution.py:20
  115.2 0.0 collective-permute-start.4
  115.2 7.1 %collective-permute-done.4 = bf16[16,16,256]{2,0,1:T(8,128)(2,1)S(1)} collective-permute-done((bf16[16,16,256]{2,0,1:T(8,128)(2,1)S(1)}, bf16[16,16,256]{2,0,1:T(8,128)(2,1)S(1)}, u32[]{:S(2)}, u32[]{:S(2)}) %collective-permute-start.4) | collective-permute-done | bytes 131104 | tf_op jit(solution)/shard_map/ppermute | solution.py:20
  122.3 0.0 collective-permute-start.5
  122.3 7.1 %collective-permute-done.5 = bf16[16,16,256]{2,0,1:T(8,128)(2,1)S(1)} collective-permute-done((bf16[16,16,256]{2,0,1:T(8,128)(2,1)S(1)}, bf16[16,16,256]{2,0,1:T(8,128)(2,1)S(1)}, u32[]{:S(2)}, u32[]{:S(2)}) %collective-permute-start.5) | collective-permute-done | bytes 131104 | tf_op jit(solution)/shard_map/ppermute | solution.py:20
  129.4 0.0 collective-permute-start.6
  129.4 7.1 %collective-permute-done.6 = bf16[16,16,256]{2,0,1:T(8,128)(2,1)S(1)} collective-permute-done((bf16[16,16,256]{2,0,1:T(8,128)(2,1)S(1)}, bf16[16,16,256]{2,0,1:T(8,128)(2,1)S(1)}, u32[]{:S(2)}, u32[]{:S(2)}) %collective-permute-start.6) | collective-permute-done | bytes 131104 | tf_op jit(solution)/shard_map/ppermute | solution.py:20
  136.5 0.0 collective-permute-start.7
  136.5 7.1 %collective-permute-done.7 = bf16[16,16,256]{2,0,1:T(8,128)(2,1)S(1)} collective-permute-done((bf16[16,16,256]{2,0,1:T(8,128)(2,1)S(1)}, bf16[16,16,256]{2,0,1:T(8,128)(2,1)S(1)}, u32[]{:S(2)}, u32[]{:S(2)}) %collective-permute-start.7) | collective-permute-done | bytes 131104 | tf_op jit(solution)/shard_map/ppermute | solution.py:20
  143.5 0.0 collective-permute-start.8
  143.6 7.1 %collective-permute-done.8 = bf16[16,16,256]{2,0,1:T(8,128)(2,1)S(1)} collective-permute-done((bf16[16,16,256]{2,0,1:T(8,128)(2,1)S(1)}, bf16[16,16,256]{2,0,1:T(8,128)(2,1)S(1)}, u32[]{:S(2)}, u32[]{:S(2)}) %collective-permute-start.8) | collective-permute-done | bytes 131104 | tf_op jit(solution)/shard_map/ppermute | solution.py:20
  150.6 0.0 collective-permute-start.9
  150.6 7.1 %collective-permute-done.9 = bf16[16,16,256]{2,0,1:T(8,128)(2,1)S(1)} collective-permute-done((bf16[16,16,256]{2,0,1:T(8,128)(2,1)S(1)}, bf16[16,16,256]{2,0,1:T(8,128)(2,1)S(1)}, u32[]{:S(2)}, u32[]{:S(2)}) %collective-permute-start.9) | collective-permute-done | bytes 131104 | tf_op jit(solution)/shard_map/ppermute | solution.py:20
  157.7 0.0 collective-permute-start.10
  157.7 7.1 %collective-permute-done.10 = bf16[16,16,256]{2,0,1:T(8,128)(2,1)S(1)} collective-permute-done((bf16[16,16,256]{2,0,1:T(8,128)(2,1)S(1)}, bf16[16,16,256]{2,0,1:T(8,128)(2,1)S(1)}, u32[]{:S(2)}, u32[]{:S(2)}) %collective-permute-start.10) | collective-permute-done | bytes 131104 | tf_op jit(solution)/shard_map/ppermute | solution.py:20
  164.8 0.0 collective-permute-start.11
  164.8 7.1 %collective-permute-done.11 = bf16[16,16,256]{2,0,1:T(8,128)(2,1)S(1)} collective-permute-done((bf16[16,16,256]{2,0,1:T(8,128)(2,1)S(1)}, bf16[16,16,256]{2,0,1:T(8,128)(2,1)S(1)}, u32[]{:S(2)}, u32[]{:S(2)}) %collective-permute-start.11) | collective-permute-done | bytes 131104 | tf_op jit(solution)/shard_map/ppermute | solution.py:20
  171.9 0.0 collective-permute-start.12
  171.9 7.1 %collective-permute-done.12 = bf16[16,16,256]{2,0,1:T(8,128)(2,1)S(1)} collective-permute-done((bf16[16,16,256]{2,0,1:T(8,128)(2,1)S(1)}, bf16[16,16,256]{2,0,1:T(8,128)(2,1)S(1)}, u32[]{:S(2)}, u32[]{:S(2)}) %collective-permute-start.12) | collective-permute-done | bytes 131104 | tf_op jit(solution)/shard_map/ppermute | solution.py:20
  179.0 0.0 collective-permute-start.13
  179.0 7.1 %collective-permute-done.13 = bf16[16,16,256]{2,0,1:T(8,128)(2,1)S(1)} collective-permute-done((bf16[16,16,256]{2,0,1:T(8,128)(2,1)S(1)}, bf16[16,16,256]{2,0,1:T(8,128)(2,1)S(1)}, u32[]{:S(2)}, u32[]{:S(2)}) %collective-permute-start.13) | collective-permute-done | bytes 131104 | tf_op jit(solution)/shard_map/ppermute | solution.py:20
  186.1 0.0 collective-permute-start.14
  186.1 0.6 dynamic_slice.11
  188.6 0.9 copy.12
  189.5 3.7 %collective-permute-done.14 = bf16[16,16,256]{2,0,1:T(8,128)(2,1)S(1)} collective-permute-done((bf16[16,16,256]{2,0,1:T(8,128)(2,1)S(1)}, bf16[16,16,256]{2,0,1:T(8,128)(2,1)S(1)}, u32[]{:S(2)}, u32[]{:S(2)}) %collective-permute-start.14) | collective-permute-done | bytes 131104 | tf_op jit(solution)/shard_map/ppermute | solution.py:20
  193.8 0.5 constant_dynamic-slice_fusion
  194.3 0.8 copy.11
  (36 shorter events, 0.4 us)
Async XLA Ops:
  0.6 36.4 %copy-start.1 = (s32[16]{0:T(128)S(1)}, s32[16]{0:T(128)}, u32[]{:S(2)}) copy-start(s32[16]{0:T(128)} %param.5) | copy-start | bytes 196
  27.9 58.7 %copy-start = (f32[16,16,256]{2,1,0:T(8,128)S(1)}, f32[16,16,256]{2,1,0:T(8,128)}, u32[]{:S(2)}) copy-start(f32[16,16,256]{2,1,0:T(8,128)} %param.4) | copy-start | bytes 786436
  29.7 15.3 %all-to-all-start = ((bf16[16,2,2048]{2,1,0:T(2,128)(2,1)}), bf16[16,2,2048]{2,1,0:T(2,128)(2,1)S(1)}, u32[]{:S(2)}, u32[]{:S(2)}) async-start(bf16[16,2,2048]{2,1,0:T(2,128)(2,1)} %reshape.8), calls=%async_computation | async-start | bytes 262144 | tf_op jit(solution)/shard_map/all_to_all | solution.py:38
  86.8 7.1 %collective-permute-start = (bf16[16,16,256]{2,0,1:T(8,128)(2,1)S(1)}, bf16[16,16,256]{2,0,1:T(8,128)(2,1)S(1)}, u32[]{:S(2)}, u32[]{:S(2)}) collective-permute-start(bf16[16,16,256]{2,0,1:T(8,128)(2,1)S(1)} %get-tuple-element.7), channel_id=1, source_target_pairs={{0,2},{2,4},{4,6},{6,8},{8,10},{10,12},{12,14},{14,16},{16,18},{18... | collective-permute-start | bytes 393224 | tf_op jit(solution)/shard_map/ppermute | solution.py:20
  93.9 7.1 %collective-permute-start.1 = (bf16[16,16,256]{2,0,1:T(8,128)(2,1)S(1)}, bf16[16,16,256]{2,0,1:T(8,128)(2,1)S(1)}, u32[]{:S(2)}, u32[]{:S(2)}) collective-permute-start(bf16[16,16,256]{2,0,1:T(8,128)(2,1)S(1)} %collective-permute-done), channel_id=1, source_target_pairs={{0,2},{2,4},{4,6},{6,8},{8,10},{10,12},{12,14},{14,16},{16,18},{18... | collective-permute-start | bytes 393224 | tf_op jit(solution)/shard_map/ppermute | solution.py:20
  101.0 7.1 %collective-permute-start.2 = (bf16[16,16,256]{2,0,1:T(8,128)(2,1)S(1)}, bf16[16,16,256]{2,0,1:T(8,128)(2,1)S(1)}, u32[]{:S(2)}, u32[]{:S(2)}) collective-permute-start(bf16[16,16,256]{2,0,1:T(8,128)(2,1)S(1)} %collective-permute-done.1), channel_id=1, source_target_pairs={{0,2},{2,4},{4,6},{6,8},{8,10},{10,12},{12,14},{14,16},{16,18},{18... | collective-permute-start | bytes 393224 | tf_op jit(solution)/shard_map/ppermute | solution.py:20
  108.1 7.1 %collective-permute-start.3 = (bf16[16,16,256]{2,0,1:T(8,128)(2,1)S(1)}, bf16[16,16,256]{2,0,1:T(8,128)(2,1)S(1)}, u32[]{:S(2)}, u32[]{:S(2)}) collective-permute-start(bf16[16,16,256]{2,0,1:T(8,128)(2,1)S(1)} %collective-permute-done.2), channel_id=1, source_target_pairs={{0,2},{2,4},{4,6},{6,8},{8,10},{10,12},{12,14},{14,16},{16,18},{18... | collective-permute-start | bytes 393224 | tf_op jit(solution)/shard_map/ppermute | solution.py:20
  115.2 7.1 %collective-permute-start.4 = (bf16[16,16,256]{2,0,1:T(8,128)(2,1)S(1)}, bf16[16,16,256]{2,0,1:T(8,128)(2,1)S(1)}, u32[]{:S(2)}, u32[]{:S(2)}) collective-permute-start(bf16[16,16,256]{2,0,1:T(8,128)(2,1)S(1)} %collective-permute-done.3), channel_id=1, source_target_pairs={{0,2},{2,4},{4,6},{6,8},{8,10},{10,12},{12,14},{14,16},{16,18},{18... | collective-permute-start | bytes 393224 | tf_op jit(solution)/shard_map/ppermute | solution.py:20
  122.3 7.1 %collective-permute-start.5 = (bf16[16,16,256]{2,0,1:T(8,128)(2,1)S(1)}, bf16[16,16,256]{2,0,1:T(8,128)(2,1)S(1)}, u32[]{:S(2)}, u32[]{:S(2)}) collective-permute-start(bf16[16,16,256]{2,0,1:T(8,128)(2,1)S(1)} %collective-permute-done.4), channel_id=1, source_target_pairs={{0,2},{2,4},{4,6},{6,8},{8,10},{10,12},{12,14},{14,16},{16,18},{18... | collective-permute-start | bytes 393224 | tf_op jit(solution)/shard_map/ppermute | solution.py:20
  129.4 7.1 %collective-permute-start.6 = (bf16[16,16,256]{2,0,1:T(8,128)(2,1)S(1)}, bf16[16,16,256]{2,0,1:T(8,128)(2,1)S(1)}, u32[]{:S(2)}, u32[]{:S(2)}) collective-permute-start(bf16[16,16,256]{2,0,1:T(8,128)(2,1)S(1)} %collective-permute-done.5), channel_id=1, source_target_pairs={{0,2},{2,4},{4,6},{6,8},{8,10},{10,12},{12,14},{14,16},{16,18},{18... | collective-permute-start | bytes 393224 | tf_op jit(solution)/shard_map/ppermute | solution.py:20
  136.5 7.1 %collective-permute-start.7 = (bf16[16,16,256]{2,0,1:T(8,128)(2,1)S(1)}, bf16[16,16,256]{2,0,1:T(8,128)(2,1)S(1)}, u32[]{:S(2)}, u32[]{:S(2)}) collective-permute-start(bf16[16,16,256]{2,0,1:T(8,128)(2,1)S(1)} %collective-permute-done.6), channel_id=1, source_target_pairs={{0,2},{2,4},{4,6},{6,8},{8,10},{10,12},{12,14},{14,16},{16,18},{18... | collective-permute-start | bytes 393224 | tf_op jit(solution)/shard_map/ppermute | solution.py:20
  143.5 7.1 %collective-permute-start.8 = (bf16[16,16,256]{2,0,1:T(8,128)(2,1)S(1)}, bf16[16,16,256]{2,0,1:T(8,128)(2,1)S(1)}, u32[]{:S(2)}, u32[]{:S(2)}) collective-permute-start(bf16[16,16,256]{2,0,1:T(8,128)(2,1)S(1)} %collective-permute-done.7), channel_id=1, source_target_pairs={{0,2},{2,4},{4,6},{6,8},{8,10},{10,12},{12,14},{14,16},{16,18},{18... | collective-permute-start | bytes 393224 | tf_op jit(solution)/shard_map/ppermute | solution.py:20
  150.6 7.1 %collective-permute-start.9 = (bf16[16,16,256]{2,0,1:T(8,128)(2,1)S(1)}, bf16[16,16,256]{2,0,1:T(8,128)(2,1)S(1)}, u32[]{:S(2)}, u32[]{:S(2)}) collective-permute-start(bf16[16,16,256]{2,0,1:T(8,128)(2,1)S(1)} %collective-permute-done.8), channel_id=1, source_target_pairs={{0,2},{2,4},{4,6},{6,8},{8,10},{10,12},{12,14},{14,16},{16,18},{18... | collective-permute-start | bytes 393224 | tf_op jit(solution)/shard_map/ppermute | solution.py:20
  157.7 7.1 %collective-permute-start.10 = (bf16[16,16,256]{2,0,1:T(8,128)(2,1)S(1)}, bf16[16,16,256]{2,0,1:T(8,128)(2,1)S(1)}, u32[]{:S(2)}, u32[]{:S(2)}) collective-permute-start(bf16[16,16,256]{2,0,1:T(8,128)(2,1)S(1)} %collective-permute-done.9), channel_id=1, source_target_pairs={{0,2},{2,4},{4,6},{6,8},{8,10},{10,12},{12,14},{14,16},{16,18},{18... | collective-permute-start | bytes 393224 | tf_op jit(solution)/shard_map/ppermute | solution.py:20
  164.8 7.1 %collective-permute-start.11 = (bf16[16,16,256]{2,0,1:T(8,128)(2,1)S(1)}, bf16[16,16,256]{2,0,1:T(8,128)(2,1)S(1)}, u32[]{:S(2)}, u32[]{:S(2)}) collective-permute-start(bf16[16,16,256]{2,0,1:T(8,128)(2,1)S(1)} %collective-permute-done.10), channel_id=1, source_target_pairs={{0,2},{2,4},{4,6},{6,8},{8,10},{10,12},{12,14},{14,16},{16,18},{18... | collective-permute-start | bytes 393224 | tf_op jit(solution)/shard_map/ppermute | solution.py:20
  171.9 7.1 %collective-permute-start.12 = (bf16[16,16,256]{2,0,1:T(8,128)(2,1)S(1)}, bf16[16,16,256]{2,0,1:T(8,128)(2,1)S(1)}, u32[]{:S(2)}, u32[]{:S(2)}) collective-permute-start(bf16[16,16,256]{2,0,1:T(8,128)(2,1)S(1)} %collective-permute-done.11), channel_id=1, source_target_pairs={{0,2},{2,4},{4,6},{6,8},{8,10},{10,12},{12,14},{14,16},{16,18},{18... | collective-permute-start | bytes 393224 | tf_op jit(solution)/shard_map/ppermute | solution.py:20
  179.0 7.1 %collective-permute-start.13 = (bf16[16,16,256]{2,0,1:T(8,128)(2,1)S(1)}, bf16[16,16,256]{2,0,1:T(8,128)(2,1)S(1)}, u32[]{:S(2)}, u32[]{:S(2)}) collective-permute-start(bf16[16,16,256]{2,0,1:T(8,128)(2,1)S(1)} %collective-permute-done.12), channel_id=1, source_target_pairs={{0,2},{2,4},{4,6},{6,8},{8,10},{10,12},{12,14},{14,16},{16,18},{18... | collective-permute-start | bytes 393224 | tf_op jit(solution)/shard_map/ppermute | solution.py:20
  186.1 7.1 %collective-permute-start.14 = (bf16[16,16,256]{2,0,1:T(8,128)(2,1)S(1)}, bf16[16,16,256]{2,0,1:T(8,128)(2,1)S(1)}, u32[]{:S(2)}, u32[]{:S(2)}) collective-permute-start(bf16[16,16,256]{2,0,1:T(8,128)(2,1)S(1)} %collective-permute-done.13), channel_id=1, source_target_pairs={{0,2},{2,4},{4,6},{6,8},{8,10},{10,12},{12,14},{14,16},{16,18},{18... | collective-permute-start | bytes 393224 | tf_op jit(solution)/shard_map/ppermute | solution.py:20
